TPU v7x, 512 devices: a whole 4x4x16 slice. The times are simulated.
512 devices in a mesh: rows: 64 (over x, y, z_hi, core), cols: 8 (over z_lo).
Axes of the slice: x: 4, y: 4, z: 16 (z_hi: 2, z_lo: 8; z = z_hi * 8 + z_lo), core: 2. Of those that a mesh axis runs over, the one named last changes fastest.
Arguments:
- homolog_embedding: bfloat16 [512, 1024, 256], P('rows', 'cols'), may hold values from -120 to 120
- couple_embedding: bfloat16 [1024, 1024, 128], P('rows', 'cols'), may hold values from -6 to 6
- homolog_standardize_factor: float32 [256], replicated, may hold values from 0.25 to 1.75
- first_factor_mapping: bfloat16 [256, 32], replicated, may hold values from -0.375 to 0.375
- second_factor_mapping: bfloat16 [256, 32], replicated, may hold values from -0.375 to 0.375
- contraction_to_couple_mapping: bfloat16 [1024, 128], replicated, may hold values from -4 to 4
- couple_standardize_factor: float32 [128], replicated, may hold values from 0.25 to 1.75
- widening_matrix: bfloat16 [128, 512], replicated, may hold values from -0.5 to 0.5
- narrowing_matrix: bfloat16 [512, 128], replicated, may hold values from -0.25 to 0.25
Outputs:
- pair_out: bfloat16 [1024, 1024, 128], P('rows', 'cols')
All inputs are finite; a program needn't handle non-finite values.
Results may differ from a plain program's by a relative error of at most 0.0064.
Values may be sent and summed in bfloat16 or wider, within the bound.
A program may use at most 64 MiB of HBM per device.

v0:
```python
import math
import jax
import jax.numpy as jnp
from jax import lax
from jax.sharding import PartitionSpec as P


def standardize_features(sampled_entries, gain_vector):
    floats = sampled_entries.astype(jnp.float32)
    average = jnp.mean(floats, axis=-1, keepdims=True)
    centred = floats - average
    variance = jnp.mean(centred * centred, axis=-1, keepdims=True)
    return centred * lax.rsqrt(variance + 1e-05) * gain_vector


def project_rows(sampled_entries, weights):
    unrolled_tensor = sampled_entries.reshape(-1, sampled_entries.shape[2])
    product = jnp.dot(unrolled_tensor, weights, preferred_element_type=jnp.float32).astype(
        jnp.bfloat16
    )
    return product.reshape(sampled_entries.shape[0], sampled_entries.shape[1], weights.shape[1])


def on_device(
    homolog_embedding,
    couple_embedding,
    homolog_standardize_factor,
    first_factor_mapping,
    second_factor_mapping,
    contraction_to_couple_mapping,
    couple_standardize_factor,
    widening_matrix,
    narrowing_matrix,
):
    standardized_tensor = standardize_features(
        homolog_embedding, homolog_standardize_factor
    ).astype(jnp.bfloat16)
    res_local = standardized_tensor.shape[1]
    width_outer = first_factor_mapping.shape[1]
    right_local = project_rows(standardized_tensor, second_factor_mapping)
    left_local = project_rows(standardized_tensor, first_factor_mapping)
    copies = jnp.tile(left_local, (1, lax.axis_size("cols"), 1))
    left_tile = lax.all_to_all(
        lax.all_to_all(copies, "cols", split_axis=1, concat_axis=1, tiled=True),
        "rows",
        split_axis=1,
        concat_axis=0,
        tiled=True,
    )
    right_panel = lax.all_gather(right_local, "rows", axis=0, tiled=True)
    sequences = left_tile.shape[0]
    tile_height = left_tile.shape[1]
    block = math.gcd(tile_height, 4)
    block_count = tile_height // block
    left_blocks = left_tile.reshape(sequences, block_count, block * width_outer).transpose(1, 0, 2)
    right_matrix = right_panel.reshape(sequences, res_local * width_outer)

    def project_block(left_block):
        outer_product = (
            lax.dot_general(
                left_block,
                right_matrix,
                (((0,), (0,)), ((), ())),
                preferred_element_type=jnp.float32,
            )
            / sequences
        )
        outer_product = outer_product.astype(jnp.bfloat16).reshape(
            block, width_outer, res_local, width_outer
        )
        outer_product = outer_product.transpose(0, 2, 1, 3).reshape(
            block * res_local, width_outer * width_outer
        )
        return jnp.dot(
            outer_product, contraction_to_couple_mapping, preferred_element_type=jnp.float32
        )

    update = lax.map(project_block, left_blocks).reshape(
        tile_height, res_local, contraction_to_couple_mapping.shape[1]
    )
    pair_mid = couple_embedding.astype(jnp.float32) + update
    pair_normed = (
        standardize_features(pair_mid, couple_standardize_factor)
        .astype(jnp.bfloat16)
        .reshape(-1, couple_embedding.shape[2])
    )
    hidden = jnp.maximum(
        jnp.dot(pair_normed, widening_matrix, preferred_element_type=jnp.float32), 0.0
    ).astype(jnp.bfloat16)
    result = pair_mid + jnp.dot(
        hidden, narrowing_matrix, preferred_element_type=jnp.float32
    ).reshape(couple_embedding.shape)
    return result.astype(jnp.bfloat16)


def solution(mesh):
    return jax.shard_map(
        on_device,
        mesh=mesh,
        in_specs=(
            P("rows", "cols", None),
            P("rows", "cols", None),
            P(),
            P(),
            P(),
            P(),
            P(),
            P(),
            P(),
        ),
        out_specs=P("rows", "cols", None),
        check_vma=False,
    )
```

profile of v0, /device:TPU:1, one launch (start us, length us, event | category | flops | bytes accessed | tf_op | source)
XLA Modules:
  0.0 234.6 jit_solution(8320753588659107767)
XLA Ops:
  12.4 2.0 reshape.66
  14.4 39.6 %all_to_all.20 = bf16[8,2,16384]{2,1,0:T(2,128)(2,1)S(1)} all-to-all(bf16[8,2,16384]{2,1,0:T(2,128)(2,1)S(1)} %reshape.66), channel_id=1, replica_groups=mesh['rows'=64,'cols'=8] {'cols'}, dimensions={0} | all-to-all | bytes 1048576 | tf_op jit(solution)/shard_map/all_to_all | solution.py:44
  56.4 4.5 %reshape.68 = bf16[64,2,2048]{2,1,0:T(2,128)(2,1)} reshape(bf16[1024,8,32]{2,1,0:T(8,128)(2,1)} %bitcast_bitcast_fusion) | data formatting | bytes 1048576
  60.9 18.2 %all-to-all-start.1 = ((bf16[64,2,2048]{2,1,0:T(2,128)(2,1)}), bf16[64,2,2048]{2,1,0:T(2,128)(2,1)}, u32[]{:S(2)}, u32[]{:S(2)}) async-start(bf16[64,2,2048]{2,1,0:T(2,128)(2,1)} %reshape.68), calls=%async_computation.1 | async-start | bytes 1048576 | tf_op jit(solution)/shard_map/all_to_all | solution.py:43
  79.1 35.0 %all-to-all-done.1 = bf16[64,2,2048]{2,1,0:T(2,128)(2,1)} async-done(((bf16[64,2,2048]{2,1,0:T(2,128)(2,1)}), bf16[64,2,2048]{2,1,0:T(2,128)(2,1)}, u32[]{:S(2)}, u32[]{:S(2)}) %all-to-all-start.1) | async-done | bytes 524320 | tf_op jit(solution)/shard_map/all_to_all | solution.py:43
  114.1 3.0 %reshape.69 = bf16[1024,8,32]{2,1,0:T(8,128)(2,1)S(1)} reshape(bf16[64,2,2048]{2,1,0:T(2,128)(2,1)} %all-to-all-done.1) | data formatting | bytes 1048576
  117.2 1.9 copy.26
  119.1 3.1 %reshape.60 = bf16[512,4,128]{2,1,0:T(4,128)(2,1)S(1)} reshape(bf16[64,8,16,32]{3,2,1,0:T(8,128)(2,1)} %copy.26) | data formatting | bytes 1048576 | tf_op jit(solution)/shard_map/reshape | solution.py:55
  122.3 40.2 %all-gather.2.cloned.1.call-done = bf16[512,128,32]{1,2,0:T(8,128)(2,1)} async-done(((bf16[8,128,32]{1,2,0:T(8,128)(2,1)}), bf16[512,128,32]{1,2,0:T(8,128)(2,1)}) %all-gather.2.cloned.1.call-update) | async-done | bytes 4194320 | tf_op jit(solution)/shard_map/all_gather | solution.py:50
  162.5 8.6 %copy.28 = bf16[512,128,32]{0,2,1:T(8,128)(2,1)} copy(bf16[512,128,32]{1,2,0:T(8,128)(2,1)} %all-gather.2.cloned.1.call-done) | data formatting | bytes 8388608 | tf_op jit(solution)/shard_map/all_gather | solution.py:50
  171.1 6.4 %copy.30 = bf16[512,4096]{1,0:T(8,128)(2,1)} copy(bf16[512,4096]{0,1:T(8,128)(2,1)} %bitcast.72) | data formatting | bytes 8388608 | tf_op jit(solution)/shard_map/while | solution.py:78
  177.5 46.2 %while.10 = (s32[]{:T(128)}, f32[4,512,128]{2,1,0:T(8,128)S(1)}, bf16[4,512,128]{2,1,0:T(8,128)(2,1)S(1)}, bf16[512,4096]{1,0:T(8,128)(2,1)}, bf16[1024,128]{1,0:T(8,128)(2,1)S(1)}, /*index=5*/s32[]{:T(128)}) while((s32[]{:T(128)}, f32[4,512,128]{2,1,0:T(8,128)S(1)}, bf16[4,512,128]{2,1,0:T(8,128)(2,1)S(1)}, bf16[512,4096]{1,0:T(8,128)(2,1)}, ...), condition=%wide.region_3.4_spmd, body=%wide.region_2.3_spmd.sunk | while | flops 672137216 | bytes 11141197 | solution.py:78
  177.5 3.0 %fusion.36 = bf16[128,4096]{1,0:T(8,128)(2,1)S(1)} fusion(bf16[512,4096]{1,0:T(8,128)(2,1)} %get-tuple-element.104, bf16[4,512,128]{2,1,0:T(8,128)(2,1)S(1)} %get-tuple-element.103, s32[]{:T(128)} %get-tuple-element.95), kind=kOutput, calls=%fused_computation.1.clone.1 | convolution fusion | flops 537919488 | bytes 5373956 | tf_op jit(solution)/shard_map/while/body/eval_jaxpr/dot_general | solution.py:60
  180.5 4.4 %reshape.71 = bf16[4,32,128,32]{3,2,1,0:T(8,128)(2,1)} reshape(bf16[128,4096]{1,0:T(8,128)(2,1)S(1)} %fusion.36) | data formatting | bytes 2097152 | tf_op jit(solution)/shard_map/while/body/eval_jaxpr/reshape | solution.py:68
  184.9 3.7 %copy.44 = bf16[4,128,32,32]{1,0,3,2:T(4,128)(2,1)S(1)} copy(bf16[4,128,32,32]{3,1,2,0:T(8,128)(2,1)} %bitcast.66) | data formatting | bytes 2097152 | tf_op jit(solution)/shard_map/while/body/eval_jaxpr/transpose | solution.py:71
  189.1 2.9 %fusion.36 = bf16[128,4096]{1,0:T(8,128)(2,1)S(1)} fusion(bf16[512,4096]{1,0:T(8,128)(2,1)} %get-tuple-element.104, bf16[4,512,128]{2,1,0:T(8,128)(2,1)S(1)} %get-tuple-element.103, s32[]{:T(128)} %get-tuple-element.95), kind=kOutput, calls=%fused_computation.1.clone.1 | convolution fusion | flops 537919488 | bytes 5373956 | tf_op jit(solution)/shard_map/while/body/eval_jaxpr/dot_general | solution.py:60
  192.1 4.4 %reshape.71 = bf16[4,32,128,32]{3,2,1,0:T(8,128)(2,1)} reshape(bf16[128,4096]{1,0:T(8,128)(2,1)S(1)} %fusion.36) | data formatting | bytes 2097152 | tf_op jit(solution)/shard_map/while/body/eval_jaxpr/reshape | solution.py:68
  196.5 3.7 %copy.44 = bf16[4,128,32,32]{1,0,3,2:T(4,128)(2,1)S(1)} copy(bf16[4,128,32,32]{3,1,2,0:T(8,128)(2,1)} %bitcast.66) | data formatting | bytes 2097152 | tf_op jit(solution)/shard_map/while/body/eval_jaxpr/transpose | solution.py:71
  200.7 2.9 %fusion.36 = bf16[128,4096]{1,0:T(8,128)(2,1)S(1)} fusion(bf16[512,4096]{1,0:T(8,128)(2,1)} %get-tuple-element.104, bf16[4,512,128]{2,1,0:T(8,128)(2,1)S(1)} %get-tuple-element.103, s32[]{:T(128)} %get-tuple-element.95), kind=kOutput, calls=%fused_computation.1.clone.1 | convolution fusion | flops 537919488 | bytes 5373956 | tf_op jit(solution)/shard_map/while/body/eval_jaxpr/dot_general | solution.py:60
  203.6 4.4 %reshape.71 = bf16[4,32,128,32]{3,2,1,0:T(8,128)(2,1)} reshape(bf16[128,4096]{1,0:T(8,128)(2,1)S(1)} %fusion.36) | data formatting | bytes 2097152 | tf_op jit(solution)/shard_map/while/body/eval_jaxpr/reshape | solution.py:68
  208.0 3.7 %copy.44 = bf16[4,128,32,32]{1,0,3,2:T(4,128)(2,1)S(1)} copy(bf16[4,128,32,32]{3,1,2,0:T(8,128)(2,1)} %bitcast.66) | data formatting | bytes 2097152 | tf_op jit(solution)/shard_map/while/body/eval_jaxpr/transpose | solution.py:71
  212.2 2.9 %fusion.36 = bf16[128,4096]{1,0:T(8,128)(2,1)S(1)} fusion(bf16[512,4096]{1,0:T(8,128)(2,1)} %get-tuple-element.104, bf16[4,512,128]{2,1,0:T(8,128)(2,1)S(1)} %get-tuple-element.103, s32[]{:T(128)} %get-tuple-element.95), kind=kOutput, calls=%fused_computation.1.clone.1 | convolution fusion | flops 537919488 | bytes 5373956 | tf_op jit(solution)/shard_map/while/body/eval_jaxpr/dot_general | solution.py:60
  215.1 4.4 %reshape.71 = bf16[4,32,128,32]{3,2,1,0:T(8,128)(2,1)} reshape(bf16[128,4096]{1,0:T(8,128)(2,1)S(1)} %fusion.36) | data formatting | bytes 2097152 | tf_op jit(solution)/shard_map/while/body/eval_jaxpr/reshape | solution.py:68
  219.6 3.7 %copy.44 = bf16[4,128,32,32]{1,0,3,2:T(4,128)(2,1)S(1)} copy(bf16[4,128,32,32]{3,1,2,0:T(8,128)(2,1)} %bitcast.66) | data formatting | bytes 2097152 | tf_op jit(solution)/shard_map/while/body/eval_jaxpr/transpose | solution.py:71
  (42 shorter events, 14.2 us)
Async XLA Ops:
  6.5 219.0 %copy-start = (bf16[512,128]{1,0:T(8,128)(2,1)S(1)}, bf16[512,128]{1,0:T(8,128)(2,1)}, u32[]{:S(2)}) copy-start(bf16[512,128]{1,0:T(8,128)(2,1)} %param.19) | copy-start | bytes 393220
  6.5 4.1 %copy-start.2 = (bf16[256,32]{0,1:T(8,128)(2,1)S(1)}, bf16[256,32]{0,1:T(8,128)(2,1)}, u32[]{:S(2)}) copy-start(bf16[256,32]{0,1:T(8,128)(2,1)} %param.15) | copy-start | bytes 49156
  6.5 5.1 %copy-start.3 = (bf16[256,32]{0,1:T(8,128)(2,1)S(1)}, bf16[256,32]{0,1:T(8,128)(2,1)}, u32[]{:S(2)}) copy-start(bf16[256,32]{0,1:T(8,128)(2,1)} %param.14) | copy-start | bytes 49156
  6.5 155.9 %all-gather.2.cloned.1.call-start = ((), (), s32[]{:S(2)}) async-start(), calls=%async_computation.2 | async-start | bytes 4259840 | tf_op jit(solution)/shard_map/all_gather | solution.py:50
  60.9 53.3 %all-to-all-start.1 = ((bf16[64,2,2048]{2,1,0:T(2,128)(2,1)}), bf16[64,2,2048]{2,1,0:T(2,128)(2,1)}, u32[]{:S(2)}, u32[]{:S(2)}) async-start(bf16[64,2,2048]{2,1,0:T(2,128)(2,1)} %reshape.68), calls=%async_computation.1 | async-start | bytes 1048576 | tf_op jit(solution)/shard_map/all_to_all | solution.py:43
  171.1 6.4 %copy-start.5 = (bf16[1024,128]{1,0:T(8,128)(2,1)S(1)}, bf16[1024,128]{1,0:T(8,128)(2,1)}, u32[]{:S(2)}) copy-start(bf16[1024,128]{1,0:T(8,128)(2,1)} %param.16) | copy-start | bytes 786436
  177.5 46.2 %copy-start.1 = (bf16[16,128,128]{2,1,0:T(8,128)(2,1)S(1)}, bf16[16,128,128]{2,1,0:T(8,128)(2,1)}, u32[]{:S(2)}) copy-start(bf16[16,128,128]{2,1,0:T(8,128)(2,1)} %param.12) | copy-start | bytes 1572868
  223.7 1.1 copy-start.4
  224.1 1.4 copy-start.6
Sparse Core Ops, SparseCore 0:
  11.7 150.7 all-gather.1
where the time goes:
time: 236 us; the launch traced here: 235 us
  waiting for transfers between devices  75.2 us (32%)
  local copies, waits for them, and re-layouts  65.6 us (28%)
  blocking collectives  39.6 us (17%)
  starting transfers between devices  18.3 us (8%)
  matrix products  15.5 us (7%)
  between operations  13.6 us (6%)
  other arithmetic  6.79 us (3%)
    all_gather x1, waiting for transfers between devices, on_device(): right_panel = lax.all_gather(right_local, 'rows', axis=0, tiled=True)  40.2 us
    all_to_all x1, blocking collectives, on_device(): lax.all_to_all(copies, 'cols', split_axis=1, concat_axis=1, tiled=True)  39.6 us
    all_to_all x1, waiting for transfers between devices, on_device(): lax.all_to_all(lax.all_to_all(copies, 'cols', split_axis=1, concat_axis=1...  35 us
    all_to_all x1, starting transfers between devices, on_device(): lax.all_to_all(lax.all_to_all(copies, 'cols', split_axis=1, concat_axis=1...  18.2 us
    reshape x4, local copies, waits for them, and re-layouts, project_block(): outer_product.astype(jnp.bfloat16)  17.7 us
    transpose x4, local copies, waits for them, and re-layouts, project_block(): outer_product.transpose(0, 2, 1, 3)  14.6 us
    unnamed x20, local copies, waits for them, and re-layouts  12 us
    dot_general x4, matrix products, project_block(): lax.dot_general(left_block, right_matrix, (((0,), (0,)), ((), ())), prefe...  11.8 us
  transfers between devices with their start and end apart: 2, of which 2 were waited for; matrix products, arithmetic and copies ran while one was open for 8% of the time, Pallas kernels for 0%

commit v1 on v0

--- a/solution.py
+++ b/solution.py
@@ -1,8 +1,25 @@
+import functools
 import math
 import jax
 import jax.numpy as jnp
 from jax import lax
 from jax.sharding import PartitionSpec as P
+
+
+def review_the_block(x_local, axis_key):
+    mixed_arr = jnp.concatenate(
+        lax.all_to_all(
+            jnp.stack([x_local] * lax.axis_size(axis_key), axis=0),
+            axis_name=axis_key,
+            split_axis=0,
+            concat_axis=0,
+        ),
+        axis=0,
+    )
+    return mixed_arr
+
+
+deliver_vectors = functools.partial(review_the_block, axis_key="rows")
 
 
 def standardize_features(sampled_entries, gain_vector):
@@ -47,7 +64,7 @@
         concat_axis=0,
         tiled=True,
     )
-    right_panel = lax.all_gather(right_local, "rows", axis=0, tiled=True)
+    right_panel = deliver_vectors(right_local)
     sequences = left_tile.shape[0]
     tile_height = left_tile.shape[1]
     block = math.gcd(tile_height, 4)

time: 236 us -> 387 us (1.64)
  the two profiles are of different devices: /device:TPU:1 before, /device:TPU:33 now
where the time goes in v1:
time: 387 us; the launch traced here: 386 us
  waiting for transfers between devices  212 us (55%)
  local copies, waits for them, and re-layouts  91.2 us (24%)
  blocking collectives  38 us (10%)
  starting transfers between devices  20.9 us (5%)
  matrix products  16.2 us (4%)
  other arithmetic  6.79 us (2%)
    all_to_all x1, waiting for transfers between devices, review_the_block(): lax.all_to_all(jnp.stack([x_local] * lax.axis_size(axis_key), axis=0), ax...  175 us
    all_to_all x1, blocking collectives, on_device(): lax.all_to_all(copies, 'cols', split_axis=1, concat_axis=1, tiled=True)  38 us
    all_to_all x1, waiting for transfers between devices, on_device(): lax.all_to_all(lax.all_to_all(copies, 'cols', split_axis=1, concat_axis=1...  37.2 us
    another operation x1, local copies, waits for them, and re-layouts, on_device(): right_matrix = right_panel.reshape(sequences, res_local * width_outer)  21.7 us
    reshape x4, local copies, waits for them, and re-layouts, project_block(): outer_product.astype(jnp.bfloat16)  17.8 us
    all_to_all x1, starting transfers between devices, on_device(): lax.all_to_all(lax.all_to_all(copies, 'cols', split_axis=1, concat_axis=1...  15.4 us
    transpose x4, local copies, waits for them, and re-layouts, project_block(): outer_product.transpose(0, 2, 1, 3)  14.6 us
    all_to_all x1, local copies, waits for them, and re-layouts, review_the_block(): lax.all_to_all(jnp.stack([x_local] * lax.axis_size(axis_key), axis=0), ax...  14.4 us
  transfers between devices with their start and end apart: 2, of which 2 were waited for; matrix products, arithmetic and copies ran while one was open for 2% of the time, Pallas kernels for 0%

profile of v1, /device:TPU:33, one launch (start us, length us, event | category | flops | bytes accessed | tf_op | source)
XLA Modules:
  0.0 385.6 jit_solution(16159264063623407399)
XLA Ops:
  7.6 38.0 %all_to_all.25 = bf16[8,2,16384]{2,1,0:T(2,128)(2,1)} all-to-all(bf16[8,2,16384]{2,1,0:T(2,128)(2,1)S(1)} %reshape.60), channel_id=1, replica_groups=mesh['rows'=64,'cols'=8] {'cols'}, dimensions={0} | all-to-all | bytes 1048576 | tf_op jit(solution)/shard_map/all_to_all | solution.py:61
  45.6 3.1 reshape.61
  50.1 4.5 %reshape.62 = bf16[64,2,2048]{2,1,0:T(2,128)(2,1)} reshape(bf16[1024,8,32]{2,1,0:T(8,128)(2,1)} %bitcast_bitcast_fusion) | data formatting | bytes 1048576
  54.6 15.4 %all-to-all-start.1 = ((bf16[64,2,2048]{2,1,0:T(2,128)(2,1)}), bf16[64,2,2048]{2,1,0:T(2,128)(2,1)S(1)}, u32[]{:S(2)}, u32[]{:S(2)}) async-start(bf16[64,2,2048]{2,1,0:T(2,128)(2,1)} %reshape.62), calls=%async_computation.1 | async-start | bytes 1048576 | tf_op jit(solution)/shard_map/all_to_all | solution.py:60
  70.3 37.2 %all-to-all-done.1 = bf16[64,2,2048]{2,1,0:T(2,128)(2,1)S(1)} async-done(((bf16[64,2,2048]{2,1,0:T(2,128)(2,1)}), bf16[64,2,2048]{2,1,0:T(2,128)(2,1)S(1)}, u32[]{:S(2)}, u32[]{:S(2)}) %all-to-all-start.1) | async-done | bytes 524320 | tf_op jit(solution)/shard_map/all_to_all | solution.py:60
  107.5 2.9 stack.3
  110.4 5.5 %all-to-all-start.2 = ((bf16[64,8,128,32]{2,3,1,0:T(8,128)(2,1)}), bf16[64,8,128,32]{2,3,1,0:T(8,128)(2,1)}, u32[]{:S(2)}, u32[]{:S(2)}) async-start(bf16[64,8,128,32]{2,3,1,0:T(8,128)(2,1)} %stack.3), calls=%async_computation.2 | async-start | bytes 8388608 | tf_op jit(solution)/shard_map/all_to_all | solution.py:11
  115.9 3.0 reshape.63
  120.9 3.1 reshape.56
  124.1 175.0 %all-to-all-done.2 = bf16[64,8,128,32]{2,3,1,0:T(8,128)(2,1)} async-done(((bf16[64,8,128,32]{2,3,1,0:T(8,128)(2,1)}), bf16[64,8,128,32]{2,3,1,0:T(8,128)(2,1)}, u32[]{:S(2)}, u32[]{:S(2)}) %all-to-all-start.2) | async-done | bytes 4194336 | tf_op jit(solution)/shard_map/all_to_all | solution.py:11
  299.1 14.4 %copy.26 = bf16[64,8,128,32]{3,2,1,0:T(8,128)(2,1)} copy(bf16[64,8,128,32]{2,3,1,0:T(8,128)(2,1)} %all-to-all-done.2) | data formatting | bytes 8388608 | tf_op jit(solution)/shard_map/all_to_all | solution.py:11
  313.5 21.7 %reshape_reshape.3 = bf16[512,4096]{1,0:T(8,128)(2,1)} reshape(bf16[64,8,128,32]{3,2,1,0:T(8,128)(2,1)} %copy.26) | data formatting | bytes 8388608 | tf_op jit(solution)/shard_map/reshape;reshape | solution.py:73
  335.3 46.3 %while.10 = (s32[]{:T(128)}, f32[4,512,128]{2,1,0:T(8,128)S(1)}, bf16[4,512,128]{2,1,0:T(8,128)(2,1)S(1)}, bf16[512,4096]{1,0:T(8,128)(2,1)}, bf16[1024,128]{1,0:T(8,128)(2,1)S(1)}, /*index=5*/s32[]{:T(128)}) while((s32[]{:T(128)}, f32[4,512,128]{2,1,0:T(8,128)S(1)}, bf16[4,512,128]{2,1,0:T(8,128)(2,1)S(1)}, bf16[512,4096]{1,0:T(8,128)(2,1)}, ...), condition=%wide.region_3.4_spmd, body=%wide.region_2.3_spmd.sunk | while | flops 672137216 | bytes 11141197 | solution.py:95
  335.3 3.0 fusion.36
  338.3 4.4 %reshape.65 = bf16[4,32,128,32]{3,2,1,0:T(8,128)(2,1)} reshape(bf16[128,4096]{1,0:T(8,128)(2,1)S(1)} %fusion.36) | data formatting | bytes 2097152 | tf_op jit(solution)/shard_map/while/body/eval_jaxpr/reshape | solution.py:85
  342.7 3.7 copy.41
  346.9 2.9 fusion.36
  349.9 4.4 %reshape.65 = bf16[4,32,128,32]{3,2,1,0:T(8,128)(2,1)} reshape(bf16[128,4096]{1,0:T(8,128)(2,1)S(1)} %fusion.36) | data formatting | bytes 2097152 | tf_op jit(solution)/shard_map/while/body/eval_jaxpr/reshape | solution.py:85
  354.3 3.7 copy.41
  358.5 2.9 fusion.36
  361.4 4.4 %reshape.65 = bf16[4,32,128,32]{3,2,1,0:T(8,128)(2,1)} reshape(bf16[128,4096]{1,0:T(8,128)(2,1)S(1)} %fusion.36) | data formatting | bytes 2097152 | tf_op jit(solution)/shard_map/while/body/eval_jaxpr/reshape | solution.py:85
  365.9 3.7 copy.41
  373.0 4.4 %reshape.65 = bf16[4,32,128,32]{3,2,1,0:T(8,128)(2,1)} reshape(bf16[128,4096]{1,0:T(8,128)(2,1)S(1)} %fusion.36) | data formatting | bytes 2097152 | tf_op jit(solution)/shard_map/while/body/eval_jaxpr/reshape | solution.py:85
  377.4 3.7 copy.41
  (42 shorter events, 20.2 us)
Async XLA Ops:
  0.0 383.4 %copy-start = (bf16[512,128]{1,0:T(8,128)(2,1)S(1)}, bf16[512,128]{1,0:T(8,128)(2,1)}, u32[]{:S(2)}) copy-start(bf16[512,128]{1,0:T(8,128)(2,1)} %param.19) | copy-start | bytes 393220
  48.6 21.3 %copy-start.3 = (bf16[256,32]{0,1:T(8,128)(2,1)S(1)}, bf16[256,32]{0,1:T(8,128)(2,1)}, u32[]{:S(2)}) copy-start(bf16[256,32]{0,1:T(8,128)(2,1)} %param.15) | copy-start | bytes 49156
  54.6 52.9 %all-to-all-start.1 = ((bf16[64,2,2048]{2,1,0:T(2,128)(2,1)}), bf16[64,2,2048]{2,1,0:T(2,128)(2,1)S(1)}, u32[]{:S(2)}, u32[]{:S(2)}) async-start(bf16[64,2,2048]{2,1,0:T(2,128)(2,1)} %reshape.62), calls=%async_computation.1 | async-start | bytes 1048576 | tf_op jit(solution)/shard_map/all_to_all | solution.py:60
  107.5 3.0 copy-start.2
  110.4 188.7 %all-to-all-start.2 = ((bf16[64,8,128,32]{2,3,1,0:T(8,128)(2,1)}), bf16[64,8,128,32]{2,3,1,0:T(8,128)(2,1)}, u32[]{:S(2)}, u32[]{:S(2)}) async-start(bf16[64,8,128,32]{2,3,1,0:T(8,128)(2,1)} %stack.3), calls=%async_computation.2 | async-start | bytes 8388608 | tf_op jit(solution)/shard_map/all_to_all | solution.py:11
  313.5 21.7 %copy-start.5 = (bf16[1024,128]{1,0:T(8,128)(2,1)S(1)}, bf16[1024,128]{1,0:T(8,128)(2,1)}, u32[]{:S(2)}) copy-start(bf16[1024,128]{1,0:T(8,128)(2,1)} %param.16) | copy-start | bytes 786436
  335.3 46.4 %copy-start.1 = (bf16[16,128,128]{2,1,0:T(8,128)(2,1)S(1)}, bf16[16,128,128]{2,1,0:T(8,128)(2,1)}, u32[]{:S(2)}) copy-start(bf16[16,128,128]{2,1,0:T(8,128)(2,1)} %param.12) | copy-start | bytes 1572868
  335.3 47.4 %copy-start.4 = (f32[128]{0:T(128)S(1)}, f32[128]{0:T(128)}, u32[]{:S(2)}) copy-start(f32[128]{0:T(128)} %param.17) | copy-start | bytes 1540
  381.6 1.8 copy-start.6
